TPU v7x, 8 devices: a whole 2x2x1 slice. The times are simulated.
8 devices in a mesh: dp: 1 (over z), tp: 8 (over x, y, core).
Axes of the slice: x: 2, y: 2, z: 1, core: 2. Of those that a mesh axis runs over, the one named last changes fastest.
Arguments:
- x: bfloat16 [1792, 5120], P(('dp', 'tp'))
- w_gate: bfloat16 [5120, 12288], P(None, 'tp')
- w_up: bfloat16 [5120, 12288], P(None, 'tp')
- w_down: bfloat16 [12288, 5120], P('tp')
Outputs:
- output: bfloat16 [1792, 5120], P(('dp', 'tp'))
All inputs are finite; a program needn't handle non-finite values.
Results may differ from a plain program's by a relative error of at most 0.016.
Values are sent between devices in bfloat16 or wider.
A program may use at most 2 GiB of HBM per device.

v0:
```python
import jax
import jax.numpy as jnp
from jax import lax
from jax.sharding import PartitionSpec as P


def solution(mesh):
    def step(x, w_gate, w_up, w_down):
        rows = lax.all_gather(x, "tp", axis=0, tiled=True)
        gate = jnp.dot(rows, w_gate, preferred_element_type=jnp.float32)
        up = jnp.dot(rows, w_up, preferred_element_type=jnp.float32)
        hidden = (jax.nn.silu(gate) * up).astype(jnp.bfloat16)
        term = jnp.dot(hidden, w_down, preferred_element_type=jnp.float32).astype(jnp.bfloat16)
        return lax.psum_scatter(term, "tp", scatter_dimension=0, tiled=True)

    return jax.shard_map(
        step,
        mesh=mesh,
        in_specs=(P(("dp", "tp"), None), P(None, "tp"), P(None, "tp"), P("tp", None)),
        out_specs=P(("dp", "tp"), None),
        check_vma=False,
    )
```

profile of v0, /device:TPU:1, one launch (start us, length us, event | category | flops | bytes accessed | tf_op | source)
XLA Modules:
  0.0 332.2 jit_solution(8549239289481338774)
XLA Ops:
  6.5 0.0 all-gather.2.cloned.1.call-start
  6.5 0.7 all-gather.2.cloned.1.call-update
  7.3 0.0 reduce-scatter.2.cloned.1.call-start
  7.3 94.8 %all-gather.2.cloned.1.call-done = bf16[1792,5120]{1,0:T(8,128)(2,1)} async-done(((bf16[224,5120]{1,0:T(8,128)(2,1)}), bf16[1792,5120]{1,0:T(8,128)(2,1)}) %all-gather.2.cloned.1.call-update) | async-done | bytes 18350096 | tf_op jit(solution)/shard_map/all_gather | solution.py:9
  102.2 0.0 slice-start
  102.2 0.0 slice-start.1
  102.2 37.6 %fusion = f32[1792,1536]{1,0:T(8,128)} fusion(bf16[1792,5120]{1,0:T(8,128)(2,1)} %all-gather.2.cloned.1.call-done, bf16[5120,1536]{1,0:T(8,128)(2,1)} %param.5), kind=kOutput, calls=%fused_computation.2 | convolution fusion | flops 28185722880 | bytes 45088768 | tf_op jit(solution)/shard_map/dot_general | solution.py:10
  139.7 0.0 slice-start.2
  139.7 0.0 slice-start.3
  139.7 38.3 %multiply_convert_fusion = bf16[1792,1536]{1,0:T(8,128)(2,1)} fusion(f32[1792,1536]{1,0:T(8,128)} %fusion, bf16[1792,5120]{1,0:T(8,128)(2,1)} %all-gather.2.cloned.1.call-done, bf16[5120,1536]{1,0:T(8,128)(2,1)} %param.6), kind=kOutput, calls=%fused_computation.1 | convolution fusion | flops 28202237952 | bytes 50593792 | tf_op jit(solution)/shard_map/dot_general | solution.py:11
  178.0 0.0 slice-done
  178.0 0.0 slice-done.1
  178.0 0.0 slice-done.2
  178.0 0.0 slice-done.3
  178.0 33.6 %convolution_convert_fusion = bf16[1792,5120]{1,0:T(8,128)(2,1)} fusion(bf16[1792,1536]{1,0:T(8,128)(2,1)} %multiply_convert_fusion, bf16[1536,5120]{1,0:T(8,128)(2,1)S(1)} %bitcast.7), kind=kOutput, calls=%fused_computation | convolution fusion | flops 28194897920 | bytes 39583744 | tf_op jit(solution)/shard_map/dot_general | solution.py:13
  211.6 0.0 reduce-scatter.2.cloned.1.call-update
  211.7 113.7 %reduce-scatter.2.cloned.1.call-done = bf16[224,5120]{1,0:T(8,128)(2,1)} async-done(((bf16[1792,5120]{1,0:T(8,128)(2,1)}), bf16[224,5120]{1,0:T(8,128)(2,1)}) %reduce-scatter.2.cloned.1.call-update) | async-done | bytes 2293776 | tf_op jit(solution)/shard_map/reduce_scatter | solution.py:14
  (1 shorter events, 0.0 us)
Async XLA Ops:
  6.5 95.6 %all-gather.2.cloned.1.call-start = ((), (), s32[]{:S(2)}) async-start(), calls=%async_computation.1 | async-start | bytes 20643840 | tf_op jit(solution)/shard_map/all_gather | solution.py:9
  7.3 318.1 %reduce-scatter.2.cloned.1.call-start = ((), (), s32[]{:S(2)}) async-start(), calls=%async_computation.2 | async-start | bytes 20643840 | tf_op jit(solution)/shard_map/reduce_scatter | solution.py:14
  102.2 75.9 %slice-start = ((s8[15728640]{0:T(1024)(128)(4,1)}), s8[4194304]{0:T(1024)(128)(4,1)S(1)}, s32[]{:S(2)}) async-start(s8[15728640]{0:T(1024)(128)(4,1)} %bitcast.6), calls=%async_computation.3 | async-start | bytes 8388608
  102.2 75.9 %slice-start.1 = ((s8[15728640]{0:T(1024)(128)(4,1)}), s8[4194304]{0:T(1024)(128)(4,1)S(1)}, s32[]{:S(2)}) async-start(s8[15728640]{0:T(1024)(128)(4,1)} %bitcast.6), calls=%async_computation.4 | async-start | bytes 8388608
  139.7 38.3 %slice-start.2 = ((s8[15728640]{0:T(1024)(128)(4,1)}), s8[4194304]{0:T(1024)(128)(4,1)S(1)}, s32[]{:S(2)}) async-start(s8[15728640]{0:T(1024)(128)(4,1)} %bitcast.6), calls=%async_computation.5 | async-start | bytes 8388608
  139.7 38.3 %slice-start.3 = ((s8[15728640]{0:T(1024)(128)(4,1)}), s8[3145728]{0:T(1024)(128)(4,1)S(1)}, s32[]{:S(2)}) async-start(s8[15728640]{0:T(1024)(128)(4,1)} %bitcast.6), calls=%async_computation.6 | async-start | bytes 6291456
Sparse Core Ops, SparseCore 0:
  9.1 92.9 all-gather.1
  211.8 113.5 reduce-scatter.1
where the time goes:
time: 334 us; the launch traced here: 332 us
  waiting for transfers between devices  209 us (63%)
  matrix products  109 us (33%)
  between operations  13.4 us (4%)
    reduce_scatter x1, waiting for transfers between devices, step(): return lax.psum_scatter(term, 'tp', scatter_dimension=0, tiled=True)  114 us
    all_gather x1, waiting for transfers between devices, step(): rows = lax.all_gather(x, 'tp', axis=0, tiled=True)  94.8 us
    dot_general x1, matrix products, step(): up = jnp.dot(rows, w_up, preferred_element_type=jnp.float32)  38.3 us
    dot_general x1, matrix products, step(): gate = jnp.dot(rows, w_gate, preferred_element_type=jnp.float32)  37.6 us
    dot_general x1, matrix products, step(): jnp.dot(hidden, w_down, preferred_element_type=jnp.float32)  33.6 us
  transfers between devices with their start and end apart: 2, of which 2 were waited for; matrix products, arithmetic and copies ran while one was open for 0% of the time, Pallas kernels for 0%

commit v1 on v0

v1 whole, which is shorter than its diff:
```python
import functools

import jax
import jax.numpy as jnp
from jax import lax
from jax.experimental import pallas as pl
from jax.experimental.pallas import tpu as pltpu
from jax.sharding import PartitionSpec as P

MESH = pl.DeviceIdType.MESH
ROWS, D, F = 224, 5120, 1536
HALF = ROWS // 2
TG, TD = 256, 512
NG, ND = F // TG, D // TD
PIECE = 16
NP = HALF // PIECE
RING = 4
BF = jnp.bfloat16
F32 = jnp.float32


def events_done(slot):
    at = (3, 4, 5, 6, 7, 7, 7, 9, 10, 11, 12, 13, 14, 15, 16, 17, 18, 19, 20, 21, 22)
    n = 0
    for a in at:
        n = n + jnp.where(slot >= a, 1, 0)
    return n


def kernel(
    x, wg, wu, wd,
    y, xo, xf, s2, sib0,
    wgv, wuv, wdv, lhs, hid, ring, obuf, sib, diag,
    w_sem, wd_sem, lhs_sem, sx_sem, sy_sem, fwd_sem, d2d_sem, xo_sem, xf_sem,
    f_send, sib_recv, o1_send, o2_send, o3_send, s2_recv, diag_recv, o3_recv, y_sem, tail_sem,
    credit, nbr_credit,
):
    me = lax.axis_index("tp")
    xn, yn, core = me ^ 4, me ^ 2, me ^ 1
    A, B = pl.ds(0, HALF), pl.ds(HALF, HALF)

    def remote(src, dst, send, recv, to):
        return pltpu.make_async_remote_copy(
            src_ref=src, dst_ref=dst, send_sem=send, recv_sem=recv,
            device_id={"tp": to}, device_id_type=MESH,
        )

    def load_lhs(src, q):
        return pltpu.make_async_copy(src, lhs.at[lax.rem(q, 2)], lhs_sem.at[lax.rem(q, 2)])

    def load_w(src, dst, t, k):
        return pltpu.make_async_copy(src.at[:, pl.ds(t * TG, TG)], dst.at[t], w_sem.at[k, t])

    def load_wd(j):
        return pltpu.make_async_copy(wd.at[:, pl.ds(j * TD, TD)], wdv.at[j], wd_sem.at[j])

    pltpu.make_async_copy(x, lhs.at[0], lhs_sem.at[0]).start()
    for t in range(NG):
        load_w(wg, wgv, t, 0).start()
        load_w(wu, wuv, t, 1).start()

    barrier = pltpu.get_barrier_semaphore()
    for other in (xn, yn, core):
        pl.semaphore_signal(barrier, inc=1, device_id={"tp": other}, device_id_type=MESH)
    pl.semaphore_wait(barrier, 3)

    def piece(h, k):
        return pl.ds(pl.multiple_of(h * HALF + k * PIECE, PIECE), PIECE)

    def own_piece(g, h, k):
        r = piece(h, k)
        over_x = (h == 0) == (g == 0)
        return remote(x.at[r], xo.at[g, r], (sx_sem if over_x else sy_sem).at[0], xo_sem.at[g, h, k],
                      xn if over_x else yn)

    @pl.loop(0, NP)
    def _(k):
        own_piece(0, 0, k).start()
        own_piece(0, 1, k).start()

    remote(x, xf.at[0], d2d_sem.at[0], xf_sem.at[0], core).start()
    for j in range(ND):
        load_wd(j).start()

    def handle(e):
        g, k = e // NP, lax.rem(e, NP)
        for h in (0, 1):
            r = piece(h, k)
            rows = xo.at[g, r]
            remote(rows, rows, sx_sem.at[0], xo_sem.at[g, h, k], xn).wait_recv()
            remote(rows, xf.at[g + 1, r], d2d_sem.at[g + 1], xf_sem.at[g + 1], core).start()

            @pl.when(g == 0)
            def _():
                remote(rows, xo.at[1, r], fwd_sem.at[h], xo_sem.at[1, h, k], yn if h == 0 else xn).start()

        @pl.when(e == NP - 1)
        def _():
            @pl.loop(0, NP)
            def _(k):
                own_piece(2, 0, k).start()
                own_piece(2, 1, k).start()

    def run_events(slot):
        lo = events_done(slot - 1)
        hi = events_done(slot)

        @pl.loop(lo, hi)
        def _(e):
            handle(e)

    def load_partner(g, q):
        remote(xf.at[g], xf.at[g], d2d_sem.at[g], xf_sem.at[g], core).wait_recv()
        load_lhs(xf.at[g], q).start()

    def gate_up(q):
        @pl.when((q >= 2) & (lax.rem(q, 2) == 0))
        def _():
            load_lhs(xo.at[q // 2 - 1], q + 1).start()

        load_lhs(x, q).wait()
        rows = lhs.at[lax.rem(q, 2)]
        dst = hid.at[jnp.minimum(q, 1)]

        @pl.loop(0, NG)
        def _(t):
            @pl.when(q == 0)
            def _():
                load_w(wg, wgv, t, 0).wait()
                load_w(wu, wuv, t, 1).wait()

                @pl.when(t == NG - 2)
                def _():
                    load_partner(0, 1)

            gate = jnp.dot(rows[...], wgv[t], preferred_element_type=F32)
            up = jnp.dot(rows[...], wuv[t], preferred_element_type=F32)
            dst[:, pl.ds(pl.multiple_of(t * TG, TG), TG)] = (jax.nn.silu(gate) * up).astype(BF)

            @pl.when(lax.rem(t, 2) == 1)
            def _():
                run_events(4 * q + t // 2)

    def down(h, j):
        return jnp.dot(hid[h], wdv[j], preferred_element_type=F32)

    def f_copy(slot, j, g):
        dst = sib0.at[j] if g == 0 else sib.at[j]
        return remote(ring.at[slot], dst, f_send.at[slot], sib_recv.at[0 if g == 0 else 1], core)

    def f_down(q):
        @pl.when(q >= 4)
        def _():
            pl.semaphore_wait(credit, 1)

        base = ND * (q // 2)

        @pl.loop(0, ND)
        def _(j):
            slot = lax.rem(base + j, RING)

            @pl.when(q == 1)
            def _():
                load_wd(j).wait()

            @pl.when(base + j >= RING)
            def _():
                f_copy(slot, j, 1).wait_send()

            ring[slot] = down(1, j).astype(BF)

            @pl.when(q == 1)
            def _():
                f_copy(slot, j, 0).start()

            @pl.when(q > 1)
            def _():
                f_copy(slot, j, 1).start()

    def wait_sib():
        remote(sib, sib, f_send.at[0], sib_recv.at[1], core).wait_recv()

    def o_copy(src, dst, send, recv, j, h, to):
        r = A if h == 0 else B
        return remote(src.at[j, r], dst.at[j, r], send, recv, to)

    def o1_copy(j, h):
        return o_copy(obuf.at[0], s2, o1_send.at[h], s2_recv.at[h], j, h, xn if h == 0 else yn)

    def o2_copy(j, h):
        return o_copy(obuf.at[1], diag, o2_send.at[h, j], diag_recv.at[h, j], j, h, xn if h == 0 else yn)

    def o3_copy(j, h):
        return o_copy(obuf.at[1], obuf.at[0], o3_send.at[h], o3_recv.at[h, j], j, h, yn if h == 0 else xn)

    def half_wait(buf, send, recv, h, which):
        r = A if h == 0 else B
        c = remote(buf.at[:, r], buf.at[:, r], send, recv, xn)
        c.wait_send() if which == "send" else c.wait_recv()

    def o_down(q):
        wait_sib()

        @pl.loop(0, ND)
        def _(j):
            obuf[jnp.where(q == 3, 0, 1), j] = (down(1, j) + sib[j].astype(F32)).astype(BF)
            for h in (0, 1):
                @pl.when(q == 3)
                def _():
                    o1_copy(j, h).start()

                @pl.when(q == 5)
                def _():
                    o2_copy(j, h).start()

        pl.semaphore_signal(credit, inc=1, device_id={"tp": core}, device_id_type=MESH)

    def o_last():
        for h in (0, 1):
            half_wait(obuf.at[0], o1_send.at[h], s2_recv.at[h], h, "send")
        for other in (xn, yn):
            pl.semaphore_signal(nbr_credit, inc=1, device_id={"tp": other}, device_id_type=MESH)
        wait_sib()
        pl.semaphore_wait(nbr_credit, 2)

        @pl.loop(0, ND)
        def _(j):
            for h in (0, 1):
                o2_copy(j, h).wait_recv()
                o2_copy(j, h).wait_send()
            acc = down(1, j) + sib[j].astype(F32) + diag[j].astype(F32)
            obuf[1, j] = acc.astype(BF)
            for h in (0, 1):
                o3_copy(j, h).start()

    @pl.loop(0, 8)
    def _(q):
        gate_up(q)

        @pl.when((q == 1) | ((q >= 2) & (lax.rem(q, 2) == 0)))
        def _():
            f_down(q)

        @pl.when((q == 3) | (q == 5))
        def _():
            o_down(q)

        run_events(4 * q + 3)

        @pl.when((q == 1) | (q == 3) | (q == 5))
        def _():
            load_partner((q + 1) // 2, q + 1)

    o_last()

    load_sib0 = pltpu.make_async_copy(sib0, sib, tail_sem.at[0])
    load_s2 = pltpu.make_async_copy(s2, diag, tail_sem.at[1])
    remote(sib0, sib0, f_send.at[0], sib_recv.at[0], core).wait_recv()
    load_sib0.start()
    for h in (0, 1):
        half_wait(s2, o1_send.at[h], s2_recv.at[h], h, "recv")
    load_s2.start()
    for s in range(RING):
        f_copy(s, 0, 1).wait_send()
    load_sib0.wait()
    load_s2.wait()

    def y_copy(j):
        slot = lax.rem(j, RING)
        return pltpu.make_async_copy(
            ring.at[slot], y.at[:, pl.ds(pl.multiple_of(j * TD, TD), TD)], y_sem.at[slot]
        )

    @pl.loop(0, ND)
    def _(j):
        @pl.when(j >= RING)
        def _():
            y_copy(j).wait()

        acc = down(0, j) + sib[j].astype(F32) + diag[j].astype(F32)
        for h in (0, 1):
            o3_copy(j, h).wait_recv()
        ring[lax.rem(j, RING)] = (acc + obuf[0, j].astype(F32)).astype(BF)
        y_copy(j).start()

    for j in range(ND - RING, ND):
        y_copy(j).wait()

    remote(x, x, sx_sem.at[0], xf_sem.at[0], xn).wait_send()
    remote(x, x, sy_sem.at[0], xf_sem.at[0], yn).wait_send()
    for h in (0, 1):
        remote(x.at[A], x.at[A], fwd_sem.at[h], xf_sem.at[0], yn).wait_send()
        half_wait(obuf.at[1], o3_send.at[h], s2_recv.at[h], h, "send")
    for g in range(4):
        remote(x, x, d2d_sem.at[g], xf_sem.at[0], core).wait_send()


def solution(mesh):
    def step(x, w_gate, w_up, w_down):
        hbm = pl.BlockSpec(memory_space=pltpu.HBM)
        shape = lambda *s: jax.ShapeDtypeStruct(s, BF)
        dma, reg = pltpu.SemaphoreType.DMA, pltpu.SemaphoreType.REGULAR
        y, *_ = pl.pallas_call(
            kernel,
            out_shape=[
                shape(ROWS, D), shape(3, ROWS, D), shape(4, ROWS, D), shape(ND, ROWS, TD), shape(ND, ROWS, TD),
            ],
            in_specs=[hbm] * 4,
            out_specs=[hbm] * 5,
            scratch_shapes=[
                pltpu.VMEM((NG, D, TG), BF), pltpu.VMEM((NG, D, TG), BF), pltpu.VMEM((ND, F, TD), BF),
                pltpu.VMEM((2, ROWS, D), BF), pltpu.VMEM((2, ROWS, F), BF), pltpu.VMEM((RING, ROWS, TD), BF),
                pltpu.VMEM((2, ND, ROWS, TD), BF), pltpu.VMEM((ND, ROWS, TD), BF), pltpu.VMEM((ND, ROWS, TD), BF),
                dma((2, NG)), dma((ND,)), dma((2,)), dma((1,)), dma((1,)), dma((2,)), dma((4,)),
                dma((3, 2, NP)), dma((4,)),
                dma((RING,)), dma((2,)), dma((2,)), dma((2, ND)), dma((2,)), dma((2,)), dma((2, ND)),
                dma((2, ND)), dma((RING,)), dma((2,)),
                reg, reg,
            ],
            compiler_params=pltpu.CompilerParams(
                collective_id=0, has_side_effects=True, vmem_limit_bytes=67043328,
            ),
            name="mlp_block",
        )(x, w_gate, w_up, w_down)
        return y

    return jax.shard_map(
        step,
        mesh=mesh,
        in_specs=(P(("dp", "tp"), None), P(None, "tp"), P(None, "tp"), P("tp", None)),
        out_specs=P(("dp", "tp"), None),
        check_vma=False,
    )
```

time: 334 us -> 158 us (0.47)
  waiting for transfers between devices: 209 us -> 0 us
  Pallas kernels: 0 us -> 153 us
  matrix products: 109 us -> 0 us
  between operations: 13.4 us -> 0.01 us
    pallas_call x0 -> x1, Pallas kernels: none -> 153 us  [step(): pl.pallas_call(kernel, out_shape=[shape(ROWS, D), shape(3, ROWS, D), shap...]
    reduce_scatter x1 -> x0, waiting for transfers between devices: 114 us -> none  [step(): return lax.psum_scatter(term, 'tp', scatter_dimension=0, tiled=True)]
    dot_general x3 -> x0, matrix products: 109 us -> none  [the longest x1 38.3 us: step(): up = jnp.dot(rows, w_up, preferred_element_type=jnp.float32)]
    all_gather x1 -> x0, waiting for transfers between devices: 94.8 us -> none  [step(): rows = lax.all_gather(x, 'tp', axis=0, tiled=True)]
  transfers between devices with their start and end apart: 2 -> 0, of which waited for: 2 -> 0; matrix products, arithmetic and copies ran while one was open for 0% -> 0% of each run, Pallas kernels for 0% -> 0%
where the time goes in v1:
time: 158 us; the launch traced here: 156 us
  Pallas kernels  153 us (97%)
  local copies, waits for them, and re-layouts  3.18 us (2%)
    pallas_call x1, Pallas kernels, step(): pl.pallas_call(kernel, out_shape=[shape(ROWS, D), shape(3, ROWS, D), shap...  153 us
    unnamed x1, local copies, waits for them, and re-layouts  3.18 us

profile of v1, /device:TPU:1, one launch (start us, length us, event | category | flops | bytes accessed | tf_op | source)
XLA Modules:
  0.0 156.2 jit_solution(1685031406433899160)
XLA Ops:
  0.0 153.1 %mlp_block.1 = (bf16[224,5120]{1,0:T(8,128)(2,1)}, bf16[3,224,5120]{2,1,0:T(8,128)(2,1)}, bf16[4,224,5120]{2,1,0:T(8,128)(2,1)}, bf16[10,224,512]{2,1,0:T(8,128)(2,1)}, bf16[10,224,512]{2,1,0:T(8,128)(2,1)}) custom-call(bf16[224,5120]{1,0:T(8,128)(2,1)} %x.1, bf16[5120,1536]{1,0:T(8,128)(2,1)} %wg.1, bf16[5120,1536]{1,0:T(8,128)(2,1)} %wu.1, ...), custom_call_target="tpu_custom_call" | custom-call | tf_op jit(solution)/shard_map/mlp_block/pallas_call | solution.py:303
  153.1 3.2 %copy.6 = bf16[224,5120]{1,0:T(8,128)(2,1)} copy(bf16[224,5120]{1,0:T(8,128)(2,1)} %get-tuple-element.6) | data formatting | bytes 4587520
